TPU v7x, 32 devices: a whole 2x2x4 slice. The times are simulated.
32 devices in a mesh: pp: 4 (over x, core), tp: 2 (over y), dp: 4 (over z).
Axes of the slice: x: 2, y: 2, z: 4, core: 2. Of those that a mesh axis runs over, the one named last changes fastest.
Arguments:
- layer_input: bfloat16 [4, 4, 16, 4096], P('pp', 'dp', 'tp'), may hold values from -4 to 4
- gate_pre: bfloat16 [4, 4, 16, 14784], P('pp', 'dp', None, 'tp'), may hold values from -8 to 8
- up_pre: bfloat16 [4, 4, 16, 14784], P('pp', 'dp', None, 'tp'), may hold values from -6 to 6
- hidden_grad: bfloat16 [4, 4, 16, 14784], P('pp', 'dp', None, 'tp'), may hold values from -0.59765625 to 0.59765625
- gate_weight: bfloat16 [4, 4096, 14784], P('pp', 'dp', 'tp'), may hold values from -0.09375 to 0.09375
Outputs:
- passed_grad: bfloat16 [4, 4, 16, 4096], P('pp', 'dp', 'tp')
- gate_weight_grad: bfloat16 [4, 4096, 14784], P('pp', 'dp', 'tp')
All inputs are finite; a program needn't handle non-finite values.
Results may differ from a plain program's by a relative error of at most 0.018.
Values may be sent and summed in bfloat16 or wider, within the bound.
No kernel may reach another device: no remote copies, remote signals or barrier semaphores. Data moves between devices by JAX's collectives and lax.ppermute only.
A program may use at most 128 MiB of HBM per device.

v0:
```python
import jax
import jax.numpy as jnp
from jax import lax
from jax.sharding import PartitionSpec as P


def from_behind(block, axis, distance):
    devices = range(lax.axis_size(axis))
    route = [(i - distance, i) for i in devices if i - distance in devices]
    return lax.ppermute(block, axis, route)


def finish(partial_value):
    return lax.psum_scatter(
        partial_value.astype(jnp.bfloat16), "tp", scatter_dimension=0, tiled=True
    )


def on_device(layer_input, gate_pre, up_pre, hidden_grad, gate_weight):
    tokens_in = layer_input[0, 0]
    gate_val = gate_pre[0, 0].astype(jnp.float32)
    up_val = up_pre[0, 0].astype(jnp.float32)
    hidden_val = hidden_grad[0, 0].astype(jnp.float32)
    gate_local = gate_weight[0]
    rows_total = gate_val.shape[0]
    groups = lax.axis_size("dp")
    logistic = jax.nn.sigmoid(gate_val)
    gate_grad = (hidden_val * up_val * logistic * (1.0 + gate_val * (1.0 - logistic))).astype(
        jnp.bfloat16
    )
    gathered_in = lax.all_gather(tokens_in, "tp", axis=0, tiled=True)
    contract_cols = (((1,), (1,)), ((), ()))
    all_grads = lax.all_gather(gate_grad, "dp", axis=0, tiled=True)
    partial_value = lax.dot_general(
        all_grads, gate_local, contract_cols, preferred_element_type=jnp.float32
    )
    returned = lax.all_to_all(
        partial_value.astype(jnp.bfloat16), "dp", split_axis=0, concat_axis=1, tiled=True
    ).astype(partial_value.dtype)
    input_grad = finish(returned)
    in_columns = lax.all_to_all(gathered_in, "dp", split_axis=1, concat_axis=0, tiled=True)
    products = lax.dot_general(
        in_columns.reshape(groups, rows_total, in_columns.shape[1]),
        all_grads.reshape(groups, rows_total, all_grads.shape[1]),
        (((1,), (1,)), ((0,), (0,))),
        preferred_element_type=jnp.float32,
    )
    rounded = lax.optimization_barrier(products.astype(jnp.bfloat16))
    grads_total = jnp.sum(rounded.astype(jnp.float32), axis=0)
    passed = from_behind(input_grad, "pp", -1)
    gate_out = grads_total.astype(jnp.bfloat16)
    return (passed[None, None], gate_out[None])


def solution(mesh):
    return jax.shard_map(
        on_device,
        mesh=mesh,
        in_specs=(
            P("pp", "dp", "tp", None),
            P("pp", "dp", None, "tp"),
            P("pp", "dp", None, "tp"),
            P("pp", "dp", None, "tp"),
            P("pp", "dp", "tp"),
        ),
        out_specs=(P("pp", "dp", "tp", None), P("pp", "dp", "tp")),
        check_vma=False,
    )
```

profile of v0, /device:TPU:0, one launch (start us, length us, event | category | flops | bytes accessed | tf_op | source)
XLA Modules:
  0.0 123.4 jit_solution(5903681675003052307)
XLA Ops:
  7.2 0.0 copy-start
  7.2 0.0 reduce-scatter.2.cloned.1.call-start
  7.2 1.4 %fusion.10 = bf16[16,7392]{1,0:T(8,128)(2,1)S(1)} fusion(bf16[1,1,16,7392]{3,2,1,0:T(8,128)(2,1)} %param.7, bf16[1,1,16,7392]{3,2,1,0:T(8,128)(2,1)} %param.8, bf16[1,1,16,7392]{3,2,1,0:T(8,128)(2,1)} %param.6), kind=kLoop, calls=%fused_computation.11 | loop fusion | flops 1537536 | bytes 946176 | tf_op jit(solution)/shard_map/convert_element_type | solution.py:28
  8.6 23.1 %all_gather.6 = bf16[64,7392]{1,0:T(8,128)(2,1)S(1)} all-gather(bf16[16,7392]{1,0:T(8,128)(2,1)S(1)} %fusion.10), channel_id=1, replica_groups=mesh['pp'=4,'tp'=2,'dp'=4] {'dp'}, dimensions={0}, use_global_device_ids=true | all-gather | bytes 1182720 | tf_op jit(solution)/shard_map/all_gather | solution.py:33
  31.7 8.0 %fusion.2 = bf16[64,1024]{1,0:T(8,128)(2,1)S(1)} fusion(bf16[64,7392]{1,0:T(8,128)(2,1)S(1)} %all_gather.6, bf16[1,1024,7392]{1,2,0:T(8,128)(2,1)} %param.9), kind=kOutput, calls=%fused_computation.3 | convolution fusion | flops 968949760 | bytes 16216064 | tf_op jit(solution)/shard_map/dot_general | solution.py:34
  39.8 9.1 %all_to_all.35 = bf16[4,16,1024]{2,1,0:T(8,128)(2,1)S(1)} all-to-all(bf16[4,16,1024]{2,1,0:T(8,128)(2,1)S(1)} %bitcast.30), channel_id=1, replica_groups=mesh['pp'=4,'tp'=2,'dp'=4] {'dp'}, dimensions={0} | all-to-all | bytes 262144 | tf_op jit(solution)/shard_map/all_to_all | solution.py:37
  48.9 0.7 copy.10
  49.5 0.0 reduce-scatter.2.cloned.1.call-update
  49.6 0.0 copy-done
  49.6 4.9 %all-gather = bf16[1,1,16,4096]{3,2,1,0:T(8,128)(2,1)S(1)} all-gather(bf16[1,1,8,4096]{3,2,1,0:T(8,128)(2,1)S(1)} %copy-done), channel_id=2, replica_groups=mesh['pp'=4,'tp'=2,'dp'=4] {'tp'}, dimensions={2}, use_global_device_ids=true | all-gather | bytes 196608 | tf_op jit(solution)/shard_map/all_gather | solution.py:31
  54.5 0.1 all_to_all.30
  54.6 0.7 copy.9
  55.3 3.3 %all-to-all-start.1 = ((bf16[16,4,1024]{2,0,1:T(8,128)(2,1)}), bf16[16,4,1024]{2,0,1:T(8,128)(2,1)S(1)}, u32[]{:S(2)}, u32[]{:S(2)}) async-start(bf16[16,4,1024]{2,0,1:T(8,128)(2,1)} %copy.9), calls=%async_computation.2 | async-start | bytes 262144 | tf_op jit(solution)/shard_map/all_to_all | solution.py:41
  58.6 0.5 reduce-scatter.2.cloned.1.call-done
  59.1 1.3 %collective-permute-start = (bf16[8,4096]{1,0:T(8,128)(2,1)}, bf16[8,4096]{1,0:T(8,128)(2,1)S(1)}, u32[]{:S(2)}, u32[]{:S(2)}) collective-permute-start(bf16[8,4096]{1,0:T(8,128)(2,1)} %reduce-scatter.2.cloned.1.call-done), channel_id=1, source_target_pairs={{8,0},{16,8},{24,16},{9,1},{17,9},{25,17},{10,2},{18,10},{26,18},{... | collective-permute-start | bytes 196616 | tf_op jit(solution)/shard_map/ppermute | solution.py:10
  60.4 4.1 %all-to-all-done.1 = bf16[16,4,1024]{2,0,1:T(8,128)(2,1)S(1)} async-done(((bf16[16,4,1024]{2,0,1:T(8,128)(2,1)}), bf16[16,4,1024]{2,0,1:T(8,128)(2,1)S(1)}, u32[]{:S(2)}, u32[]{:S(2)}) %all-to-all-start.1) | async-done | bytes 131104 | tf_op jit(solution)/shard_map/all_to_all | solution.py:41
  64.5 23.4 %convert_bitcast_fusion = bf16[4,1024,7392]{1,2,0:T(8,128)(2,1)} fusion(bf16[4,16,7392]{2,1,0:T(8,128)(2,1)S(1)} %bitcast.28, bf16[16,4,1024]{2,0,1:T(8,128)(2,1)S(1)} %all-to-all-done.1), kind=kOutput, calls=%fused_computation | convolution fusion | flops 999161856 | bytes 61632512 | tf_op jit(solution)/shard_map/dot_general | solution.py:42
  87.9 28.0 %reduce_sum.12 = bf16[1024,7392]{0,1:T(8,128)(2,1)} reduce(bf16[4,1024,7392]{1,2,0:T(8,128)(2,1)} %convert_bitcast_fusion, bf16[]{:T(256)} %constant.4.clone.1), dimensions={0}, to_apply=%region_1.0 | reduce | flops 22708224 | bytes 75694080 | tf_op jit(solution)/shard_map/reduce_sum | solution.py:49
  115.9 0.0 collective-permute-done
  115.9 0.6 copy.12
Async XLA Ops:
  7.2 42.4 %copy-start = (bf16[1,1,8,4096]{3,2,1,0:T(8,128)(2,1)S(1)}, bf16[1,1,8,4096]{3,2,1,0:T(8,128)(2,1)}, u32[]{:S(2)}) copy-start(bf16[1,1,8,4096]{3,2,1,0:T(8,128)(2,1)} %param.5) | copy-start | bytes 196612
  7.2 51.9 %reduce-scatter.2.cloned.1.call-start = ((), (), s32[]{:S(2)}) async-start(), calls=%async_computation.3 | async-start | bytes 196608 | tf_op jit(solution)/shard_map/reduce_scatter | solution.py:14
  55.3 9.2 %all-to-all-start.1 = ((bf16[16,4,1024]{2,0,1:T(8,128)(2,1)}), bf16[16,4,1024]{2,0,1:T(8,128)(2,1)S(1)}, u32[]{:S(2)}, u32[]{:S(2)}) async-start(bf16[16,4,1024]{2,0,1:T(8,128)(2,1)} %copy.9), calls=%async_computation.2 | async-start | bytes 262144 | tf_op jit(solution)/shard_map/all_to_all | solution.py:41
  59.1 56.8 %collective-permute-start = (bf16[8,4096]{1,0:T(8,128)(2,1)}, bf16[8,4096]{1,0:T(8,128)(2,1)S(1)}, u32[]{:S(2)}, u32[]{:S(2)}) collective-permute-start(bf16[8,4096]{1,0:T(8,128)(2,1)} %reduce-scatter.2.cloned.1.call-done), channel_id=1, source_target_pairs={{8,0},{16,8},{24,16},{9,1},{17,9},{25,17},{10,2},{18,10},{26,18},{... | collective-permute-start | bytes 196616 | tf_op jit(solution)/shard_map/ppermute | solution.py:10
Sparse Core Ops, SparseCore 0:
  49.7 9.3 reduce-scatter.1
where the time goes:
time: 124 us; the launch traced here: 123 us
  blocking collectives  37.1 us (30%)
  matrix products  31.5 us (25%)
  other arithmetic  29.4 us (24%)
  between operations  14.1 us (11%)
  starting transfers between devices  4.64 us (4%)
  waiting for transfers between devices  4.62 us (4%)
  local copies, waits for them, and re-layouts  2.05 us (2%)
    reduce_sum x1, other arithmetic, on_device(): grads_total = jnp.sum(rounded.astype(jnp.float32), axis=0)  28 us
    dot_general x1, matrix products, on_device(): lax.dot_general(in_columns.reshape(groups, rows_total, in_columns.shape[1...  23.4 us
    all_gather x1, blocking collectives, on_device(): all_grads = lax.all_gather(gate_grad, 'dp', axis=0, tiled=True)  23.1 us
    all_to_all x1, blocking collectives, on_device(): lax.all_to_all(partial_value.astype(jnp.bfloat16), 'dp', split_axis=0, co...  9.09 us
    dot_general x1, matrix products, on_device(): lax.dot_general(all_grads, gate_local, contract_cols, preferred_element_t...  8.04 us
    all_gather x1, blocking collectives, on_device(): gathered_in = lax.all_gather(tokens_in, 'tp', axis=0, tiled=True)  4.93 us
    all_to_all x1, waiting for transfers between devices, on_device(): lax.all_to_all(gathered_in, 'dp', split_axis=1, concat_axis=0, tiled=True)  4.06 us
    all_to_all x1, starting transfers between devices, on_device(): lax.all_to_all(gathered_in, 'dp', split_axis=1, concat_axis=0, tiled=True)  3.32 us
  transfers between devices with their start and end apart: 3, of which 2 were waited for; matrix products, arithmetic and copies ran while one was open for 42% of the time, Pallas kernels for 0%

commit v1 on v0

--- a/solution.py
+++ b/solution.py
@@ -30,7 +30,12 @@
     )
     gathered_in = lax.all_gather(tokens_in, "tp", axis=0, tiled=True)
     contract_cols = (((1,), (1,)), ((), ()))
-    all_grads = lax.all_gather(gate_grad, "dp", axis=0, tiled=True)
+    ring = [gate_grad]
+    for hop in range(3):
+        ring.append(lax.ppermute(ring[-1], "dp", [(dev, (dev + 1) % 4) for dev in range(4)]))
+    all_grads = jnp.roll(
+        jnp.concatenate(ring[::-1], axis=0), (lax.axis_index("dp") + 1) * ring[0].shape[0], axis=0
+    )
     partial_value = lax.dot_general(
         all_grads, gate_local, contract_cols, preferred_element_type=jnp.float32
     )

time: 124 us -> 128 us (1.032)
  waiting for transfers between devices: 4.62 us -> 29.1 us
  blocking collectives: 37.1 us -> 13.2 us
  starting transfers between devices: 4.64 us -> 7.75 us
    ppermute x0 -> x3, waiting for transfers between devices: none -> 24.4 us  [on_device(): lax.ppermute(ring[-1], 'dp', [(dev, (dev + 1) % 4) for dev in range(4)])]
    all_gather x1 -> x0, blocking collectives: 23.1 us -> none  [on_device(): all_grads = lax.all_gather(gate_grad, 'dp', axis=0, tiled=True)]
    ppermute x0 -> x3, starting transfers between devices: none -> 3.11 us  [on_device(): lax.ppermute(ring[-1], 'dp', [(dev, (dev + 1) % 4) for dev in range(4)])]
  transfers between devices with their start and end apart: 3 -> 6, of which waited for: 2 -> 5; matrix products, arithmetic and copies ran while one was open for 42% -> 41% of each run, Pallas kernels for 0% -> 0%
where the time goes in v1:
time: 128 us; the launch traced here: 127 us
  matrix products  31.5 us (25%)
  other arithmetic  29.4 us (23%)
  waiting for transfers between devices  29.1 us (23%)
  between operations  14.1 us (11%)
  blocking collectives  13.2 us (10%)
  starting transfers between devices  7.75 us (6%)
  local copies, waits for them, and re-layouts  2.28 us (2%)
    reduce_sum x1, other arithmetic, on_device(): grads_total = jnp.sum(rounded.astype(jnp.float32), axis=0)  28 us
    ppermute x3, waiting for transfers between devices, on_device(): lax.ppermute(ring[-1], 'dp', [(dev, (dev + 1) % 4) for dev in range(4)])  24.4 us
    dot_general x1, matrix products, on_device(): lax.dot_general(in_columns.reshape(groups, rows_total, in_columns.shape[1...  23.4 us
    all_to_all x1, blocking collectives, on_device(): lax.all_to_all(partial_value.astype(jnp.bfloat16), 'dp', split_axis=0, co...  8.31 us
    dot_general x1, matrix products, on_device(): lax.dot_general(all_grads, gate_local, contract_cols, preferred_element_t...  8.08 us
    all_gather x1, blocking collectives, on_device(): gathered_in = lax.all_gather(tokens_in, 'tp', axis=0, tiled=True)  4.93 us
    all_to_all x1, waiting for transfers between devices, on_device(): lax.all_to_all(gathered_in, 'dp', split_axis=1, concat_axis=0, tiled=True)  4.28 us
    all_to_all x1, starting transfers between devices, on_device(): lax.all_to_all(gathered_in, 'dp', split_axis=1, concat_axis=0, tiled=True)  3.32 us
  transfers between devices with their start and end apart: 6, of which 5 were waited for; matrix products, arithmetic and copies ran while one was open for 41% of the time, Pallas kernels for 0%

profile of v1, /device:TPU:0, one launch (start us, length us, event | category | flops | bytes accessed | tf_op | source)
XLA Modules:
  0.0 127.4 jit_solution(12091201179701221902)
XLA Ops:
  7.2 0.0 reduce-scatter.2.cloned.1.call-start
  7.2 1.4 %fusion.10 = bf16[16,7392]{1,0:T(8,128)(2,1)S(1)} fusion(bf16[1,1,16,7392]{3,2,1,0:T(8,128)(2,1)} %param.7, bf16[1,1,16,7392]{3,2,1,0:T(8,128)(2,1)} %param.8, bf16[1,1,16,7392]{3,2,1,0:T(8,128)(2,1)} %param.6), kind=kLoop, calls=%fused_computation.11 | loop fusion | flops 1537536 | bytes 946176 | tf_op jit(solution)/shard_map/convert_element_type | solution.py:28
  8.6 3.1 %collective-permute-start = (bf16[16,7392]{1,0:T(8,128)(2,1)S(1)}, bf16[16,7392]{1,0:T(8,128)(2,1)S(1)}, u32[]{:S(2)}, u32[]{:S(2)}) collective-permute-start(bf16[16,7392]{1,0:T(8,128)(2,1)S(1)} %fusion.10), channel_id=1, source_target_pairs={{0,1},{1,2},{2,3},{3,0},{4,5},{5,6},{6,7},{7,4},{8,9},{9,10},{10,1... | collective-permute-start | bytes 709640 | tf_op jit(solution)/shard_map/ppermute | solution.py:35
  11.7 7.8 %collective-permute-done = bf16[16,7392]{1,0:T(8,128)(2,1)S(1)} collective-permute-done((bf16[16,7392]{1,0:T(8,128)(2,1)S(1)}, bf16[16,7392]{1,0:T(8,128)(2,1)S(1)}, u32[]{:S(2)}, u32[]{:S(2)}) %collective-permute-start) | collective-permute-done | bytes 236576 | tf_op jit(solution)/shard_map/ppermute | solution.py:35
  19.5 0.0 collective-permute-start.1
  19.5 8.7 %collective-permute-done.1 = bf16[16,7392]{1,0:T(8,128)(2,1)S(1)} collective-permute-done((bf16[16,7392]{1,0:T(8,128)(2,1)S(1)}, bf16[16,7392]{1,0:T(8,128)(2,1)S(1)}, u32[]{:S(2)}, u32[]{:S(2)}) %collective-permute-start.1) | collective-permute-done | bytes 236576 | tf_op jit(solution)/shard_map/ppermute | solution.py:35
  28.3 0.0 collective-permute-start.2
  28.3 7.9 %collective-permute-done.2 = bf16[16,7392]{1,0:T(8,128)(2,1)S(1)} collective-permute-done((bf16[16,7392]{1,0:T(8,128)(2,1)S(1)}, bf16[16,7392]{1,0:T(8,128)(2,1)S(1)}, u32[]{:S(2)}, u32[]{:S(2)}) %collective-permute-start.2) | collective-permute-done | bytes 236576 | tf_op jit(solution)/shard_map/ppermute | solution.py:35
  36.4 0.1 constant_dynamic-slice_fusion
  36.4 0.0 copy-start
  36.5 8.1 %fusion.2 = bf16[64,1024]{1,0:T(8,128)(2,1)S(1)} fusion(bf16[64,7392]{1,0:T(8,128)(2,1)S(1)} %constant_dynamic-slice_fusion, bf16[1,1024,7392]{1,2,0:T(8,128)(2,1)} %param.9), kind=kOutput, calls=%fused_computation.3 | convolution fusion | flops 968949760 | bytes 16216064 | tf_op jit(solution)/shard_map/dot_general | solution.py:39
  44.5 8.3 %all_to_all.35 = bf16[4,16,1024]{2,1,0:T(8,128)(2,1)S(1)} all-to-all(bf16[4,16,1024]{2,1,0:T(8,128)(2,1)S(1)} %bitcast.30), channel_id=1, replica_groups=mesh['pp'=4,'tp'=2,'dp'=4] {'dp'}, dimensions={0} | all-to-all | bytes 262144 | tf_op jit(solution)/shard_map/all_to_all | solution.py:42
  52.8 0.7 copy.10
  53.5 0.0 reduce-scatter.2.cloned.1.call-update
  53.5 0.0 copy-done
  53.5 4.9 %all-gather = bf16[1,1,16,4096]{3,2,1,0:T(8,128)(2,1)S(1)} all-gather(bf16[1,1,8,4096]{3,2,1,0:T(8,128)(2,1)S(1)} %copy-done), channel_id=2, replica_groups=mesh['pp'=4,'tp'=2,'dp'=4] {'tp'}, dimensions={2}, use_global_device_ids=true | all-gather | bytes 196608 | tf_op jit(solution)/shard_map/all_gather | solution.py:31
  58.5 0.1 all_to_all.30
  58.6 0.7 copy.9
  59.2 3.3 %all-to-all-start.1 = ((bf16[16,4,1024]{2,0,1:T(8,128)(2,1)}), bf16[16,4,1024]{2,0,1:T(8,128)(2,1)S(1)}, u32[]{:S(2)}, u32[]{:S(2)}) async-start(bf16[16,4,1024]{2,0,1:T(8,128)(2,1)} %copy.9), calls=%async_computation.2 | async-start | bytes 262144 | tf_op jit(solution)/shard_map/all_to_all | solution.py:46
  62.6 0.3 reduce-scatter.2.cloned.1.call-done
  62.9 1.3 %collective-permute-start.3 = (bf16[8,4096]{1,0:T(8,128)(2,1)}, bf16[8,4096]{1,0:T(8,128)(2,1)S(1)}, u32[]{:S(2)}, u32[]{:S(2)}) collective-permute-start(bf16[8,4096]{1,0:T(8,128)(2,1)} %reduce-scatter.2.cloned.1.call-done), channel_id=1, source_target_pairs={{8,0},{16,8},{24,16},{9,1},{17,9},{25,17},{10,2},{18,10},{26,18},{... | collective-permute-start | bytes 196616 | tf_op jit(solution)/shard_map/ppermute | solution.py:10
  64.2 4.3 %all-to-all-done.1 = bf16[16,4,1024]{2,0,1:T(8,128)(2,1)S(1)} async-done(((bf16[16,4,1024]{2,0,1:T(8,128)(2,1)}), bf16[16,4,1024]{2,0,1:T(8,128)(2,1)S(1)}, u32[]{:S(2)}, u32[]{:S(2)}) %all-to-all-start.1) | async-done | bytes 131104 | tf_op jit(solution)/shard_map/all_to_all | solution.py:46
  68.5 23.4 %convert_bitcast_fusion = bf16[4,1024,7392]{1,2,0:T(8,128)(2,1)} fusion(bf16[4,16,7392]{2,1,0:T(8,128)(2,1)S(1)} %bitcast.28, bf16[16,4,1024]{2,0,1:T(8,128)(2,1)S(1)} %all-to-all-done.1), kind=kOutput, calls=%fused_computation | convolution fusion | flops 999161856 | bytes 61632512 | tf_op jit(solution)/shard_map/dot_general | solution.py:47
  91.9 28.0 %reduce_sum.12 = bf16[1024,7392]{0,1:T(8,128)(2,1)} reduce(bf16[4,1024,7392]{1,2,0:T(8,128)(2,1)} %convert_bitcast_fusion, bf16[]{:T(256)} %constant.34.clone.1), dimensions={0}, to_apply=%region_1.2 | reduce | flops 22708224 | bytes 75694080 | tf_op jit(solution)/shard_map/reduce_sum | solution.py:54
  119.9 0.0 collective-permute-done.3
  119.9 0.6 copy.19
  (8 shorter events, 0.1 us)
Async XLA Ops:
  7.2 55.7 %reduce-scatter.2.cloned.1.call-start = ((), (), s32[]{:S(2)}) async-start(), calls=%async_computation.3 | async-start | bytes 196608 | tf_op jit(solution)/shard_map/reduce_scatter | solution.py:14
  8.6 10.9 %collective-permute-start = (bf16[16,7392]{1,0:T(8,128)(2,1)S(1)}, bf16[16,7392]{1,0:T(8,128)(2,1)S(1)}, u32[]{:S(2)}, u32[]{:S(2)}) collective-permute-start(bf16[16,7392]{1,0:T(8,128)(2,1)S(1)} %fusion.10), channel_id=1, source_target_pairs={{0,1},{1,2},{2,3},{3,0},{4,5},{5,6},{6,7},{7,4},{8,9},{9,10},{10,1... | collective-permute-start | bytes 709640 | tf_op jit(solution)/shard_map/ppermute | solution.py:35
  19.5 8.7 %collective-permute-start.1 = (bf16[16,7392]{1,0:T(8,128)(2,1)S(1)}, bf16[16,7392]{1,0:T(8,128)(2,1)S(1)}, u32[]{:S(2)}, u32[]{:S(2)}) collective-permute-start(bf16[16,7392]{1,0:T(8,128)(2,1)S(1)} %collective-permute-done), channel_id=1, source_target_pairs={{0,1},{1,2},{2,3},{3,0},{4,5},{5,6},{6,7},{7,4},{8,9},{9,10},{10,1... | collective-permute-start | bytes 709640 | tf_op jit(solution)/shard_map/ppermute | solution.py:35
  28.3 7.9 %collective-permute-start.2 = (bf16[16,7392]{1,0:T(8,128)(2,1)S(1)}, bf16[16,7392]{1,0:T(8,128)(2,1)S(1)}, u32[]{:S(2)}, u32[]{:S(2)}) collective-permute-start(bf16[16,7392]{1,0:T(8,128)(2,1)S(1)} %collective-permute-done.1), channel_id=1, source_target_pairs={{0,1},{1,2},{2,3},{3,0},{4,5},{5,6},{6,7},{7,4},{8,9},{9,10},{10,1... | collective-permute-start | bytes 709640 | tf_op jit(solution)/shard_map/ppermute | solution.py:35
  36.4 17.1 %copy-start = (bf16[1,1,8,4096]{3,2,1,0:T(8,128)(2,1)S(1)}, bf16[1,1,8,4096]{3,2,1,0:T(8,128)(2,1)}, u32[]{:S(2)}) copy-start(bf16[1,1,8,4096]{3,2,1,0:T(8,128)(2,1)} %param.5) | copy-start | bytes 196612
  59.2 9.2 %all-to-all-start.1 = ((bf16[16,4,1024]{2,0,1:T(8,128)(2,1)}), bf16[16,4,1024]{2,0,1:T(8,128)(2,1)S(1)}, u32[]{:S(2)}, u32[]{:S(2)}) async-start(bf16[16,4,1024]{2,0,1:T(8,128)(2,1)} %copy.9), calls=%async_computation.2 | async-start | bytes 262144 | tf_op jit(solution)/shard_map/all_to_all | solution.py:46
  62.9 57.0 %collective-permute-start.3 = (bf16[8,4096]{1,0:T(8,128)(2,1)}, bf16[8,4096]{1,0:T(8,128)(2,1)S(1)}, u32[]{:S(2)}, u32[]{:S(2)}) collective-permute-start(bf16[8,4096]{1,0:T(8,128)(2,1)} %reduce-scatter.2.cloned.1.call-done), channel_id=1, source_target_pairs={{8,0},{16,8},{24,16},{9,1},{17,9},{25,17},{10,2},{18,10},{26,18},{... | collective-permute-start | bytes 196616 | tf_op jit(solution)/shard_map/ppermute | solution.py:10
Sparse Core Ops, SparseCore 0:
  53.7 9.2 reduce-scatter.1
